TPU v7x, 256 devices: a 4x2x16 block of a 4x16x16 slice. The times are simulated.
256 devices in a mesh: grp: 2 (over y), slab: 32 (over z, core), ang: 4 (over x).
Axes of the slice: x: 4, y: 2, z: 16, core: 2. Of those that a mesh axis runs over, the one named last changes fastest.
The devices are a block of a 4x16x16 slice.
Arguments:
- volume: bfloat16 [128, 256, 1024], P(('grp', 'slab')), parts along dimension 0, may hold values from -6 to 6
- ray_weights: bfloat16 [8, 1024, 1024], P('ang'), may hold values from -0.0234375 to 0.0234375
- row_offsets: int32 [8, 64], P('ang'), may hold values from 0 to 8
- measured: float32 [16, 256, 1024], P(('grp', 'ang'), 'slab'), parts along dimension 0, may hold values from -6 to 6
- shifts: float32 [16], P(('grp', 'ang')), parts along dimension 0, may hold values from -4 to 4
Outputs:
- updated_volume: bfloat16 [128, 256, 1024], P(('grp', 'slab')), parts along dimension 0
- last_residual: float32 [16, 256, 1024], P(('grp', 'ang'), 'slab'), parts along dimension 0
- shift_slope: float32 [16], P(('grp', 'ang')), parts along dimension 0
There are 2 independent parts, one for each index of `grp`. A program takes and returns all parts, laid end to end along the dimension named above; an argument that names none is the same for every part. Nothing has to cross between parts.
All inputs are finite; a program needn't handle non-finite values.
Results may differ from a plain program's by a relative error of at most 0.006.
Values may be sent and summed in bfloat16 or wider, within the bound.
No kernel may reach another device: no remote copies, remote signals or barrier semaphores. Data moves between devices by JAX's collectives and lax.ppermute only.
A program may use at most 128 MiB of HBM per device.

v0:
```python
import math
import jax
import jax.numpy as jnp
from jax import lax
from jax.sharding import Mesh
from jax.sharding import PartitionSpec as P

Y = 256
X = 1024
U = 1024
OFF = 8
ROUNDS = 2
SLAB = ("slab_0", "slab_1")
GRP_SLAB = ("grp", "slab_0", "slab_1")
step_size = 0.5


def own_block(tiles, axes, order):
    lengths = [lax.axis_size(a) for a in axes]
    tiles = tiles.reshape(*lengths, *tiles.shape[1:])
    tiles = tiles.transpose(*order, *range(len(axes), tiles.ndim))
    tiles = tiles.reshape(-1, *tiles.shape[len(axes) :])
    for k in order:
        tiles = lax.psum_scatter(tiles, axes[k], scatter_dimension=0, tiled=True)
    return tiles[0]


def in_blocks(shard, dim, length):
    lengths = shard.shape
    tiles = shard.reshape(*lengths[:dim], length, lengths[dim] // length, *lengths[dim + 1 :])
    return jnp.moveaxis(tiles, dim, 0)


def summed_rows(shard, axes, order, dim):
    length = lax.axis_size(axes)
    return own_block(in_blocks(shard, dim, length), axes, order)


def in_order(tiles, dim):
    lengths = list(tiles.shape[1:])
    lengths[dim] *= tiles.shape[0]
    return jnp.moveaxis(tiles, 0, dim).reshape(lengths)


def stacked_from(shard, axes, order):
    tiles = shard
    for k in order:
        tiles = lax.all_gather(tiles, axes[k])
    done = order[::-1]
    back = [done.index(k) for k in range(len(axes))]
    tiles = tiles.transpose(*back, *range(len(axes), tiles.ndim))
    return tiles.reshape(-1, *shard.shape)


def gather_axes(shard, axes, order, dim):
    return in_order(stacked_from(shard, axes, order), dim)


def from_everyone(shard, axis):
    copies = jnp.broadcast_to(shard, (lax.axis_size(axis), *shard.shape))
    return lax.all_to_all(copies, axis, split_axis=0, concat_axis=0, tiled=True)


def over_copies(shard, axis):
    return from_everyone(shard, axis).sum(axis=0)


def move_down(products, tilt_table):
    base = jnp.zeros((products.shape[1] + OFF, U), jnp.float32)
    placed = jax.vmap(
        lambda block, shift_rows: lax.dynamic_update_slice(base, block, (shift_rows, jnp.int32(0)))
    )(products, tilt_table)
    return jnp.sum(placed, axis=0)


def backproject(extended, tilt_table, ray_weights, band_rows):
    slices_count = tilt_table.shape[1]
    running = jnp.zeros((slices_count * band_rows, X), jnp.float32)
    for angle_index in range(ray_weights.shape[0]):
        source = extended[angle_index]
        picked = jax.vmap(
            lambda shift_rows: lax.dynamic_slice(source, (shift_rows, jnp.int32(0)), (band_rows, U))
        )(tilt_table[angle_index])
        running = running + lax.dot_general(
            picked.reshape(slices_count * band_rows, U),
            ray_weights[angle_index],
            (((1,), (1,)), ((), ())),
            preferred_element_type=jnp.float32,
        )
    return running


def apply_update(current, running):
    partial_value = lax.optimization_barrier(running.reshape(current.shape).astype(jnp.bfloat16))
    partial_wide = partial_value.astype(jnp.float32)
    gradient = lax.psum(partial_wide, "ang")
    renewed = (current.astype(jnp.float32) - step_size * gradient).astype(jnp.bfloat16)
    return renewed


def per_device(volume, ray_weights, row_offsets, measured, shifts):
    angles_here = ray_weights.shape[0]
    band_rows = measured.shape[1]
    highest = lax.Precision.HIGHEST
    numbers = lax.iota(jnp.int32, U)
    turns = numbers[:, None] * numbers[None, :] % U
    radians = turns.astype(jnp.float32) * (2.0 * math.pi / U)
    cosine = jnp.cos(radians)
    sine = jnp.sin(radians)
    signed = jnp.where(numbers <= (U - 1) // 2, numbers, numbers - U)
    omega = signed.astype(jnp.float32) * (2.0 * math.pi / U)
    flat_rows = measured.reshape(angles_here * band_rows, U)
    real_part = jnp.dot(flat_rows, cosine, precision=highest).reshape(angles_here, band_rows, U)
    imag_part = -jnp.dot(flat_rows, sine, precision=highest).reshape(angles_here, band_rows, U)
    phase = omega[None, None, :] * shifts[:, None, None]
    turned_real = real_part * jnp.cos(phase) + imag_part * jnp.sin(phase)
    turned_imag = imag_part * jnp.cos(phase) - real_part * jnp.sin(phase)
    first_half = jnp.concatenate([turned_real, omega * turned_imag], axis=0).reshape(-1, U)
    second_half = jnp.concatenate([turned_imag, -omega * turned_real], axis=0).reshape(-1, U)
    inverse = (
        jnp.dot(first_half, cosine, precision=highest)
        - jnp.dot(second_half, sine, precision=highest)
    ) / U
    inverse = inverse.reshape(2, angles_here, band_rows, U)
    shifted = inverse[0]
    slope_field = inverse[1]
    projection = shifted
    residual = shifted
    current = volume
    slices_here = volume.shape[0]
    tilt_table = lax.dynamic_slice_in_dim(
        row_offsets, lax.axis_index(SLAB) * slices_here, slices_here, 1
    )
    for round_index in range(ROUNDS):
        flattened = current.reshape(slices_here * Y, X)
        partials = jnp.stack(
            [
                move_down(
                    jnp.dot(
                        flattened, ray_weights[angle_index], preferred_element_type=jnp.float32
                    ).reshape(slices_here, Y, U),
                    tilt_table[angle_index],
                )[:Y]
                for angle_index in range(angles_here)
            ]
        )
        projection = summed_rows(partials, SLAB, (1, 0), 1)
        residual = projection - shifted
        rounded = residual.astype(jnp.bfloat16)
        gathered = gather_axes(rounded, SLAB, (0, 1), 1)
        extended = jnp.concatenate(
            [gathered, jnp.zeros((angles_here, OFF, U), jnp.bfloat16)], axis=1
        )
        running = backproject(extended, tilt_table, ray_weights, Y)
        current = apply_update(current, running)
    local_dot = jnp.sum(projection * slope_field, axis=(1, 2))
    shift_slope = over_copies(local_dot, SLAB) / math.sqrt(Y * U)
    return (current, residual, shift_slope)


def solution(mesh):
    split = Mesh(
        mesh.devices.reshape(mesh.shape["grp"], 16, 2, mesh.shape["ang"]),
        ("grp", "slab_0", "slab_1", "ang"),
    )
    placed = (
        P(GRP_SLAB, None, None),
        P("ang", None, None),
        P("ang", None),
        P(("grp", "ang"), SLAB, None),
        P(("grp", "ang")),
    )
    return jax.shard_map(
        per_device,
        mesh=split,
        in_specs=placed,
        out_specs=(P(GRP_SLAB, None, None), P(("grp", "ang"), SLAB, None), P(("grp", "ang"))),
        check_vma=False,
    )
```

profile of v0, /device:TPU:34, one launch (start us, length us, event | category | flops | bytes accessed | tf_op | source)
XLA Modules:
  0.0 536.4 jit_solution(7147799609888639398)
XLA Ops:
  7.3 4.7 fusion.16
  12.0 2.6 fusion.8
  15.2 18.0 %while.12 = (s32[]{:T(128)}, f32[2,264,1024]{2,1,0:T(8,128)S(1)}, s32[2,3]{1,0:T(2,128)S(1)}, f32[2,256,1024]{2,1,0:T(8,128)}, s32[]{:T(128)}, /*index=5*/s32[3]{0:T(128)S(1)}, s32[]{:T(128)}) while((s32[]{:T(128)}, f32[2,264,1024]{2,1,0:T(8,128)S(1)}, s32[2,3]{1,0:T(2,128)S(1)}, f32[2,256,1024]{2,1,0:T(8,128)}, s32[]{:T(128)}, ...), condition=%wide.while_cond.4, body=%wide.while_body.4.sunk | while | flops 262163 | bytes 5243051 | solution.py:71
  15.9 2.8 and_reduce_fusion.8
  18.7 3.4 dynamic-slice_select_fusion.8
  22.1 2.1 dynamic-update-slice.32
  24.9 2.8 and_reduce_fusion.8
  27.7 3.4 dynamic-slice_select_fusion.8
  31.1 2.1 dynamic-update-slice.32
  33.3 1.6 broadcast.122.clone.1
  34.9 24.1 %while.13 = (s32[]{:T(128)}, f32[2,264,1024]{2,1,0:T(8,128)}, s32[2,3]{1,0:T(2,128)S(1)}, f32[2,256,1024]{2,1,0:T(8,128)}, s32[]{:T(128)}, /*index=5*/s32[3]{0:T(128)S(1)}, s32[]{:T(128)}) while((s32[]{:T(128)}, f32[2,264,1024]{2,1,0:T(8,128)}, s32[2,3]{1,0:T(2,128)S(1)}, f32[2,256,1024]{2,1,0:T(8,128)}, s32[]{:T(128)}, /*index=5*/s32[3]{0:T(128)S(1)}, ...), condition=%wide.while_cond.5, body=%wide.while_body.5.sunk | while | flops 262163 | bytes 5243051 | solution.py:71
  35.6 2.7 and_reduce_fusion.9
  38.3 3.6 dynamic-slice_select_fusion.9
  41.9 5.1 dynamic-update-slice.33
  47.6 2.7 and_reduce_fusion.9
  50.3 3.6 dynamic-slice_select_fusion.9
  53.9 5.1 dynamic-update-slice.33
  59.3 1.9 reduce_sum.55
  61.7 1.5 copy.68
  63.3 32.5 %reduce-scatter.5.cloned.1.call-done = f32[16,2,8,1024]{3,2,1,0:T(8,128)} async-done(((f32[32,2,8,1024]{3,2,1,0:T(8,128)}), f32[16,2,8,1024]{3,2,1,0:T(8,128)}) %reduce-scatter.5.cloned.1.call-update) | async-done | bytes 1048592 | tf_op jit(solution)/shard_map/reduce_scatter | solution.py:24
  96.4 17.8 %fusion.50 = f32[2,8,1024]{2,1,0:T(8,128)S(1)} fusion(f32[2,8,1024]{2,1,0:T(8,128)S(1)} %copy-done), kind=kOutput, calls=%fused_computation.67 | convolution fusion | flops 216006656 | bytes 131072 | tf_op jit(solution)/shard_map/dot_general | solution.py:113
  114.3 18.0 %broadcast_multiply_fusion = (f32[2,8,1024]{2,1,0:T(8,128)S(1)}, f32[2,8,1024]{2,1,0:T(8,128)S(1)}, f32[2,8,1024]{2,1,0:T(8,128)S(1)}, f32[2,8,1024]{2,1,0:T(8,128)S(1)}) fusion(f32[1024]{0:T(1024)S(1)} %get-tuple-element.358, f32[2,1024]{1,0:T(2,128)S(1)} %get-tuple-element.348, f32[2,8,1024]{2,1,0:T(8,128)S(1)} %fusion.50, ...), kind=kOutput, calls=%fused_computation.102 | convolution fusion | flops 216154112 | bytes 417792 | tf_op jit(solution)/shard_map/dot_general | solution.py:114
  132.3 18.4 %fusion.24 = f32[32,1024]{1,0:T(8,128)S(1)} fusion(f32[2,8,1024]{2,1,0:T(8,128)S(1)} %get-tuple-element.345, f32[2,8,1024]{2,1,0:T(8,128)S(1)} %get-tuple-element.324), kind=kOutput, calls=%fused_computation.53 | convolution fusion | flops 417366016 | bytes 262144 | tf_op jit(solution)/shard_map/dot_general | solution.py:121
  150.7 18.0 %fusion.47 = f32[32,1024]{1,0:T(8,128)S(1)} fusion(f32[32,1024]{1,0:T(8,128)S(1)} %fusion.24, f32[2,8,1024]{2,1,0:T(8,128)S(1)} %get-tuple-element.323, f32[2,8,1024]{2,1,0:T(8,128)S(1)} %get-tuple-element.346), kind=kOutput, calls=%fused_computation.66 | convolution fusion | flops 417431552 | bytes 393216 | tf_op jit(solution)/shard_map/dot_general | solution.py:122
  169.2 0.8 fusion.69
  170.0 34.9 %all_gather.20 = bf16[16,2,8,1024]{3,2,1,0:T(8,128)(2,1)} all-gather(bf16[1,2,8,1024]{3,2,1,0:T(8,128)(2,1)S(1)} %fusion.69), channel_id=1, replica_groups=mesh['grp'=2,'slab_0'=16,'slab_1'=2,'ang'=4] {'slab_0'}, dimensions={0}, use_global_device_ids=true | all-gather | bytes 557056 | tf_op jit(solution)/shard_map/all_gather | solution.py:48
  205.3 15.5 %all-gather.5.cloned.1.call-done = bf16[32,2,8,1024]{3,2,1,0:T(8,128)(2,1)} async-done(((bf16[16,2,8,1024]{3,2,1,0:T(8,128)(2,1)}), bf16[32,2,8,1024]{3,2,1,0:T(8,128)(2,1)}) %all-gather.5.cloned.1.call-update) | async-done | bytes 1048592 | tf_op jit(solution)/shard_map/all_gather | solution.py:48
  220.7 1.3 copy.69
  223.0 4.2 fusion.10
  227.8 3.5 add_convert_fusion.1
  231.3 42.2 %all-reduce.6 = f32[2,256,1024]{2,1,0:T(8,128)S(1)} all-reduce(bf16[2,256,1024]{2,1,0:T(8,128)(2,1)S(1)} %bitcast.233), channel_id=1, replica_groups=mesh['grp'=2,'slab_0'=16,'slab_1'=2,'ang'=4] {'ang'}, use_global_device_ids=true, to_apply=%region_6.7 | all-reduce | flops 524288 | bytes 3145728 | tf_op jit(solution)/shard_map/psum | solution.py:96
  273.5 1.7 subtract_convert_fusion.1
  275.3 0.8 copy-done.11
  276.0 2.6 fusion.14
  278.6 2.6 fusion.6
  281.5 17.7 %while.14 = (s32[]{:T(128)}, f32[2,264,1024]{2,1,0:T(8,128)S(1)}, s32[2,3]{1,0:T(2,128)S(1)}, f32[2,256,1024]{2,1,0:T(8,128)}, s32[]{:T(128)}, /*index=5*/s32[3]{0:T(128)S(1)}, s32[]{:T(128)}) while((s32[]{:T(128)}, f32[2,264,1024]{2,1,0:T(8,128)S(1)}, s32[2,3]{1,0:T(2,128)S(1)}, f32[2,256,1024]{2,1,0:T(8,128)}, s32[]{:T(128)}, ...), condition=%wide.while_cond.6, body=%wide.while_body.6.sunk | while | flops 262163 | bytes 5243051 | solution.py:71
  282.2 2.7 and_reduce_fusion.10
  284.9 3.3 dynamic-slice_select_fusion.10
  288.2 2.1 dynamic-update-slice.34
  291.0 2.7 and_reduce_fusion.10
  293.7 3.3 dynamic-slice_select_fusion.10
  297.0 2.1 dynamic-update-slice.34
  299.4 1.0 slice_bitcast_fusion.1
  300.7 18.1 %while.15 = (s32[]{:T(128)}, f32[2,264,1024]{2,1,0:T(8,128)S(1)}, s32[2,3]{1,0:T(2,128)S(1)}, f32[2,256,1024]{2,1,0:T(8,128)}, s32[]{:T(128)}, /*index=5*/s32[3]{0:T(128)S(1)}, s32[]{:T(128)}) while((s32[]{:T(128)}, f32[2,264,1024]{2,1,0:T(8,128)S(1)}, s32[2,3]{1,0:T(2,128)S(1)}, f32[2,256,1024]{2,1,0:T(8,128)}, s32[]{:T(128)}, ...), condition=%wide.while_cond.7, body=%wide.while_body.7.sunk | while | flops 262163 | bytes 5243051 | solution.py:71
  301.4 2.8 and_reduce_fusion.11
  304.2 3.4 dynamic-slice_select_fusion.11
  307.6 2.1 dynamic-update-slice.35
  310.4 2.8 and_reduce_fusion.11
  313.2 3.4 dynamic-slice_select_fusion.11
  316.6 2.1 dynamic-update-slice.35
  319.2 1.1 copy-done.2
  320.5 1.5 copy.75
  322.2 20.0 %reduce-scatter.9.cloned.1.call-done = f32[16,2,8,1024]{3,2,1,0:T(8,128)} async-done(((f32[32,2,8,1024]{3,2,1,0:T(8,128)}), f32[16,2,8,1024]{3,2,1,0:T(8,128)}) %reduce-scatter.9.cloned.1.call-update) | async-done | bytes 1048592 | tf_op jit(solution)/shard_map/reduce_scatter | solution.py:24
  342.3 73.3 %reduce-scatter.11.cloned.1.call-done = f32[1,2,8,1024]{3,2,1,0:T(8,128)} async-done(((f32[16,2,8,1024]{3,2,1,0:T(8,128)}), f32[1,2,8,1024]{3,2,1,0:T(8,128)}) %reduce-scatter.11.cloned.1.call-update) | async-done | bytes 65552 | tf_op jit(solution)/shard_map/reduce_scatter | solution.py:24
  415.6 0.8 fusion.70
  416.4 32.8 %all_gather.23 = bf16[16,2,8,1024]{3,2,1,0:T(8,128)(2,1)} all-gather(bf16[1,2,8,1024]{3,2,1,0:T(8,128)(2,1)S(1)} %fusion.70), channel_id=1, replica_groups=mesh['grp'=2,'slab_0'=16,'slab_1'=2,'ang'=4] {'slab_0'}, dimensions={0}, use_global_device_ids=true | all-gather | bytes 557056 | tf_op jit(solution)/shard_map/all_gather | solution.py:48
  449.3 1.5 fusion.68
  451.4 10.5 %all-to-all-start = ((f32[32,1,2]{2,1,0:T(1,128)}), f32[32,1,2]{2,1,0:T(1,128)S(1)}, u32[]{:S(2)}, u32[]{:S(2)}) async-start(f32[32,1,2]{2,1,0:T(1,128)} %broadcast_in_dim.7), calls=%async_computation.4 | async-start | bytes 32768 | tf_op jit(solution)/shard_map/all_to_all | solution.py:61
  461.9 12.1 %all-to-all-done = f32[32,1,2]{2,1,0:T(1,128)S(1)} async-done(((f32[32,1,2]{2,1,0:T(1,128)}), f32[32,1,2]{2,1,0:T(1,128)S(1)}, u32[]{:S(2)}, u32[]{:S(2)}) %all-to-all-start) | async-done | bytes 288 | tf_op jit(solution)/shard_map/all_to_all | solution.py:61
  474.6 1.3 copy.76
  476.7 4.2 fusion.12
  481.5 4.5 add_convert_fusion
  486.0 42.0 %all-reduce.7 = f32[2,256,1024]{2,1,0:T(8,128)S(1)} all-reduce(bf16[2,256,1024]{2,1,0:T(8,128)(2,1)} %bitcast.234), channel_id=1, replica_groups=mesh['grp'=2,'slab_0'=16,'slab_1'=2,'ang'=4] {'ang'}, use_global_device_ids=true, to_apply=%region_13.14 | all-reduce | flops 524288 | bytes 3145728 | tf_op jit(solution)/shard_map/psum | solution.py:96
  528.0 1.3 subtract_convert_fusion
  (106 shorter events, 15.4 us)
Async XLA Ops:
  7.2 89.2 %copy-start = (f32[2,8,1024]{2,1,0:T(8,128)S(1)}, f32[2,8,1024]{2,1,0:T(8,128)}, u32[]{:S(2)}) copy-start(f32[2,8,1024]{2,1,0:T(8,128)} %param.8) | copy-start | bytes 196612
  7.2 88.6 %reduce-scatter.5.cloned.1.call-start = ((), (), s32[]{:S(2)}) async-start(), calls=%async_computation.5 | async-start | bytes 3145728 | tf_op jit(solution)/shard_map/reduce_scatter | solution.py:24
  7.3 4.7 copy-start.5
  7.3 4.7 copy-start.10
  12.0 2.6 copy-start.7
  12.0 2.7 copy-start.8
  14.6 0.7 copy-start.6
  63.1 33.1 %copy-start.9 = (f32[2]{0:T(128)S(1)}, f32[2]{0:T(128)}, u32[]{:S(2)}) copy-start(f32[2]{0:T(128)} %param.9) | copy-start | bytes 28
  63.2 106.0 %reduce-scatter.7.cloned.1.call-start = ((), (), s32[]{:S(2)}) async-start(), calls=%async_computation.6 | async-start | bytes 1114112 | tf_op jit(solution)/shard_map/reduce_scatter | solution.py:24
  95.8 124.9 %all-gather.5.cloned.1.call-start = ((), (), s32[]{:S(2)}) async-start(), calls=%async_computation.9 | async-start | bytes 1572864 | tf_op jit(solution)/shard_map/all_gather | solution.py:48
  205.0 137.2 %reduce-scatter.9.cloned.1.call-start = ((), (), s32[]{:S(2)}) async-start(), calls=%async_computation.7 | async-start | bytes 3145728 | tf_op jit(solution)/shard_map/reduce_scatter | solution.py:24
  273.5 2.5 copy-start.11
  276.0 2.6 copy-start.3
  319.0 1.2 copy-start.2
  322.1 93.5 %reduce-scatter.11.cloned.1.call-start = ((), (), s32[]{:S(2)}) async-start(), calls=%async_computation.8 | async-start | bytes 1114112 | tf_op jit(solution)/shard_map/reduce_scatter | solution.py:24
  342.3 132.4 %all-gather.7.cloned.1.call-start = ((), (), s32[]{:S(2)}) async-start(), calls=%async_computation.10 | async-start | bytes 1572864 | tf_op jit(solution)/shard_map/all_gather | solution.py:48
  451.4 22.6 %all-to-all-start = ((f32[32,1,2]{2,1,0:T(1,128)}), f32[32,1,2]{2,1,0:T(1,128)S(1)}, u32[]{:S(2)}, u32[]{:S(2)}) async-start(f32[32,1,2]{2,1,0:T(1,128)} %broadcast_in_dim.7), calls=%async_computation.4 | async-start | bytes 32768 | tf_op jit(solution)/shard_map/all_to_all | solution.py:61
  486.0 42.0 %copy-start.4 = (bf16[2,256,1024]{2,1,0:T(8,128)(2,1)S(1)}, bf16[2,256,1024]{2,1,0:T(8,128)(2,1)}, u32[]{:S(2)}) copy-start(bf16[2,256,1024]{2,1,0:T(8,128)(2,1)} %copy-done.3) | copy-start | bytes 3145732
  486.0 43.4 %copy-start.1 = (f32[2,8,1024]{2,1,0:T(8,128)S(1)}, f32[2,8,1024]{2,1,0:T(8,128)}, u32[]{:S(2)}) copy-start(f32[2,8,1024]{2,1,0:T(8,128)} %param.8) | copy-start | bytes 196612
Sparse Core Ops, SparseCore 0:
  63.3 32.4 reduce-scatter.4
  98.3 70.8 reduce-scatter.6
  205.1 15.5 all-gather.4
  322.2 19.9 reduce-scatter.8
  344.6 70.9 reduce-scatter.10
  449.5 16.1 all-gather.6
where the time goes:
time: 542 us; the launch traced here: 536 us
  waiting for transfers between devices  154 us (28%)
  blocking collectives  152 us (28%)
  matrix products  101 us (19%)
  other arithmetic  59.6 us (11%)
  local copies, waits for them, and re-layouts  43 us (8%)
  between operations  14.8 us (3%)
  starting transfers between devices  11.1 us (2%)
    reduce_scatter x4, waiting for transfers between devices, own_block(): tiles = lax.psum_scatter(tiles, axes[k], scatter_dimension=0, tiled=True)  126 us
    psum x2, blocking collectives, apply_update(): gradient = lax.psum(partial_wide, 'ang')  84.2 us
    all_gather x2, blocking collectives, stacked_from(): tiles = lax.all_gather(tiles, axes[k])  67.7 us
    scatter x16, other arithmetic  49.3 us
    scatter x24, local copies, waits for them, and re-layouts  28.3 us
    dot_general x1, matrix products, per_device(): jnp.dot(first_half, cosine, precision=highest)  18.4 us
    dot_general x1, matrix products, per_device(): jnp.dot(flat_rows, sine, precision=highest)  18 us
    dot_general x1, matrix products, per_device(): jnp.dot(second_half, sine, precision=highest)  18 us
  transfers between devices with their start and end apart: 7, of which 6 were waited for; matrix products, arithmetic and copies ran while one was open for 14% of the time, Pallas kernels for 0%

commit v1 on v0

--- a/solution.py
+++ b/solution.py
@@ -93,7 +93,9 @@
 def apply_update(current, running):
     partial_value = lax.optimization_barrier(running.reshape(current.shape).astype(jnp.bfloat16))
     partial_wide = partial_value.astype(jnp.float32)
-    gradient = lax.psum(partial_wide, "ang")
+    gradient = partial_wide
+    for hop in (1, 2):
+        gradient = gradient + lax.ppermute(gradient, "ang", [(dev, dev ^ hop) for dev in range(4)])
     renewed = (current.astype(jnp.float32) - step_size * gradient).astype(jnp.bfloat16)
     return renewed
 

time: 542 us -> 644 us (1.19)
  waiting for transfers between devices: 154 us -> 319 us
  blocking collectives: 152 us -> 92.2 us
    ppermute x0 -> x4, waiting for transfers between devices: none -> 160 us  [apply_update(): lax.ppermute(gradient, 'ang', [(dev, dev ^ hop) for dev in range(4)])]
    psum x2 -> x0, blocking collectives: 84.2 us -> none  [apply_update(): gradient = lax.psum(partial_wide, 'ang')]
    all_to_all x0 -> x1, blocking collectives: none -> 24.7 us  [from_everyone(): return lax.all_to_all(copies, axis, split_axis=0, concat_axis=0, tiled=True)]
    all_gather x2, waiting for transfers between devices: 15.5 us -> 32.3 us  [stacked_from(): tiles = lax.all_gather(tiles, axes[k])]
    all_to_all x1 -> x0, waiting for transfers between devices: 12.1 us -> none  [from_everyone(): return lax.all_to_all(copies, axis, split_axis=0, concat_axis=0, tiled=True)]
    all_to_all x1 -> x0, starting transfers between devices: 10.5 us -> none  [from_everyone(): return lax.all_to_all(copies, axis, split_axis=0, concat_axis=0, tiled=True)]
    ppermute x0 -> x4, starting transfers between devices: none -> 7.18 us  [apply_update(): lax.ppermute(gradient, 'ang', [(dev, dev ^ hop) for dev in range(4)])]
  transfers between devices with their start and end apart: 7 -> 10, of which waited for: 6 -> 10; matrix products, arithmetic and copies ran while one was open for 14% -> 12% of each run, Pallas kernels for 0% -> 0%
where the time goes in v1:
time: 644 us; the launch traced here: 638 us
  waiting for transfers between devices  319 us (50%)
  matrix products  100 us (16%)
  blocking collectives  92.2 us (14%)
  other arithmetic  62.1 us (10%)
  local copies, waits for them, and re-layouts  41.3 us (6%)
  between operations  14.8 us (2%)
  starting transfers between devices  7.85 us (1%)
    ppermute x4, waiting for transfers between devices, apply_update(): lax.ppermute(gradient, 'ang', [(dev, dev ^ hop) for dev in range(4)])  160 us
    reduce_scatter x4, waiting for transfers between devices, own_block(): tiles = lax.psum_scatter(tiles, axes[k], scatter_dimension=0, tiled=True)  126 us
    all_gather x2, blocking collectives, stacked_from(): tiles = lax.all_gather(tiles, axes[k])  67.4 us
    scatter x16, other arithmetic  49.3 us
    all_gather x2, waiting for transfers between devices, stacked_from(): tiles = lax.all_gather(tiles, axes[k])  32.3 us
    scatter x24, local copies, waits for them, and re-layouts  27.9 us
    all_to_all x1, blocking collectives, from_everyone(): return lax.all_to_all(copies, axis, split_axis=0, concat_axis=0, tiled=True)  24.7 us
    dot_general x1, matrix products, per_device(): jnp.dot(first_half, cosine, precision=highest)  18.4 us
  transfers between devices with their start and end apart: 10, of which 10 were waited for; matrix products, arithmetic and copies ran while one was open for 12% of the time, Pallas kernels for 0%

profile of v1, /device:TPU:34, one launch (start us, length us, event | category | flops | bytes accessed | tf_op | source)
XLA Modules:
  0.0 638.3 jit_solution(14561922477371433828)
XLA Ops:
  7.3 4.6 fusion.16
  12.0 2.6 fusion.8
  15.2 17.6 %while.12 = (s32[]{:T(128)}, f32[2,264,1024]{2,1,0:T(8,128)S(1)}, s32[2,3]{1,0:T(2,128)S(1)}, f32[2,256,1024]{2,1,0:T(8,128)}, s32[]{:T(128)}, /*index=5*/s32[3]{0:T(128)S(1)}, s32[]{:T(128)}) while((s32[]{:T(128)}, f32[2,264,1024]{2,1,0:T(8,128)S(1)}, s32[2,3]{1,0:T(2,128)S(1)}, f32[2,256,1024]{2,1,0:T(8,128)}, s32[]{:T(128)}, ...), condition=%wide.while_cond.4, body=%wide.while_body.4.sunk | while | flops 262163 | bytes 5243051 | solution.py:71
  15.9 2.6 and_reduce_fusion.8
  18.5 3.4 dynamic-slice_select_fusion.8
  21.9 2.1 dynamic-update-slice.32
  24.7 2.6 and_reduce_fusion.8
  27.3 3.4 dynamic-slice_select_fusion.8
  30.7 2.1 dynamic-update-slice.32
  32.9 1.6 broadcast.122.clone.1
  34.5 24.3 %while.13 = (s32[]{:T(128)}, f32[2,264,1024]{2,1,0:T(8,128)}, s32[2,3]{1,0:T(2,128)S(1)}, f32[2,256,1024]{2,1,0:T(8,128)}, s32[]{:T(128)}, /*index=5*/s32[3]{0:T(128)S(1)}, s32[]{:T(128)}) while((s32[]{:T(128)}, f32[2,264,1024]{2,1,0:T(8,128)}, s32[2,3]{1,0:T(2,128)S(1)}, f32[2,256,1024]{2,1,0:T(8,128)}, s32[]{:T(128)}, /*index=5*/s32[3]{0:T(128)S(1)}, ...), condition=%wide.while_cond.5, body=%wide.while_body.5.sunk | while | flops 262163 | bytes 5243051 | solution.py:71
  35.2 2.7 and_reduce_fusion.9
  37.9 3.7 dynamic-slice_select_fusion.9
  41.7 5.0 dynamic-update-slice.33
  47.4 2.7 and_reduce_fusion.9
  50.1 3.7 dynamic-slice_select_fusion.9
  53.8 5.0 dynamic-update-slice.33
  59.1 1.9 reduce_sum.55
  61.5 1.5 copy.68
  63.1 32.5 %reduce-scatter.5.cloned.1.call-done = f32[16,2,8,1024]{3,2,1,0:T(8,128)} async-done(((f32[32,2,8,1024]{3,2,1,0:T(8,128)}), f32[16,2,8,1024]{3,2,1,0:T(8,128)}) %reduce-scatter.5.cloned.1.call-update) | async-done | bytes 1048592 | tf_op jit(solution)/shard_map/reduce_scatter | solution.py:24
  96.3 17.8 %fusion.50 = f32[2,8,1024]{2,1,0:T(8,128)S(1)} fusion(f32[2,8,1024]{2,1,0:T(8,128)S(1)} %copy-done), kind=kOutput, calls=%fused_computation.67 | convolution fusion | flops 216006656 | bytes 131072 | tf_op jit(solution)/shard_map/dot_general | solution.py:115
  114.1 18.0 %broadcast_multiply_fusion = (f32[2,8,1024]{2,1,0:T(8,128)S(1)}, f32[2,8,1024]{2,1,0:T(8,128)S(1)}, f32[2,8,1024]{2,1,0:T(8,128)S(1)}, f32[2,8,1024]{2,1,0:T(8,128)S(1)}) fusion(f32[1024]{0:T(1024)S(1)} %get-tuple-element.358, f32[2,1024]{1,0:T(2,128)S(1)} %get-tuple-element.348, f32[2,8,1024]{2,1,0:T(8,128)S(1)} %fusion.50, ...), kind=kOutput, calls=%fused_computation.104 | convolution fusion | flops 216154112 | bytes 417792 | tf_op jit(solution)/shard_map/dot_general | solution.py:116
  132.2 18.4 %fusion.24 = f32[32,1024]{1,0:T(8,128)S(1)} fusion(f32[2,8,1024]{2,1,0:T(8,128)S(1)} %get-tuple-element.345, f32[2,8,1024]{2,1,0:T(8,128)S(1)} %get-tuple-element.324), kind=kOutput, calls=%fused_computation.53 | convolution fusion | flops 417366016 | bytes 262144 | tf_op jit(solution)/shard_map/dot_general | solution.py:123
  150.6 18.0 %fusion.47 = f32[32,1024]{1,0:T(8,128)S(1)} fusion(f32[32,1024]{1,0:T(8,128)S(1)} %fusion.24, f32[2,8,1024]{2,1,0:T(8,128)S(1)} %get-tuple-element.323, f32[2,8,1024]{2,1,0:T(8,128)S(1)} %get-tuple-element.346), kind=kOutput, calls=%fused_computation.66 | convolution fusion | flops 417431552 | bytes 393216 | tf_op jit(solution)/shard_map/dot_general | solution.py:124
  170.0 34.8 %all_gather.20 = bf16[16,2,8,1024]{3,2,1,0:T(8,128)(2,1)} all-gather(bf16[1,2,8,1024]{3,2,1,0:T(8,128)(2,1)S(1)} %fusion.69), channel_id=1, replica_groups=mesh['grp'=2,'slab_0'=16,'slab_1'=2,'ang'=4] {'slab_0'}, dimensions={0}, use_global_device_ids=true | all-gather | bytes 557056 | tf_op jit(solution)/shard_map/all_gather | solution.py:48
  205.1 15.5 %all-gather.5.cloned.1.call-done = bf16[32,2,8,1024]{3,2,1,0:T(8,128)(2,1)} async-done(((bf16[16,2,8,1024]{3,2,1,0:T(8,128)(2,1)}), bf16[32,2,8,1024]{3,2,1,0:T(8,128)(2,1)}) %all-gather.5.cloned.1.call-update) | async-done | bytes 1048592 | tf_op jit(solution)/shard_map/all_gather | solution.py:48
  220.6 1.3 copy.69
  222.9 4.2 fusion.10
  227.6 3.5 add_convert_fusion.1
  231.4 1.4 collective-permute-start
  232.8 46.6 %collective-permute-done = f32[2,256,1024]{2,1,0:T(8,128)S(1)} collective-permute-done((f32[2,256,1024]{2,1,0:T(8,128)S(1)}, f32[2,256,1024]{2,1,0:T(8,128)S(1)}, u32[]{:S(2)}, u32[]{:S(2)}) %collective-permute-start) | collective-permute-done | bytes 2097184 | tf_op jit(solution)/shard_map/ppermute | solution.py:98
  279.7 2.2 collective-permute-start.1
  281.9 46.5 %collective-permute-done.1 = f32[2,256,1024]{2,1,0:T(8,128)} collective-permute-done((f32[2,256,1024]{2,1,0:T(8,128)S(1)}, f32[2,256,1024]{2,1,0:T(8,128)}, u32[]{:S(2)}, u32[]{:S(2)}) %collective-permute-start.1) | collective-permute-done | bytes 2097184 | tf_op jit(solution)/shard_map/ppermute | solution.py:98
  328.4 2.2 subtract_convert_fusion.1
  330.6 2.6 fusion.14
  333.2 2.6 fusion.6
  336.0 17.7 %while.14 = (s32[]{:T(128)}, f32[2,264,1024]{2,1,0:T(8,128)S(1)}, s32[2,3]{1,0:T(2,128)S(1)}, f32[2,256,1024]{2,1,0:T(8,128)}, s32[]{:T(128)}, /*index=5*/s32[3]{0:T(128)S(1)}, s32[]{:T(128)}) while((s32[]{:T(128)}, f32[2,264,1024]{2,1,0:T(8,128)S(1)}, s32[2,3]{1,0:T(2,128)S(1)}, f32[2,256,1024]{2,1,0:T(8,128)}, s32[]{:T(128)}, ...), condition=%wide.while_cond.6, body=%wide.while_body.6.sunk | while | flops 262163 | bytes 5243051 | solution.py:71
  336.7 2.7 and_reduce_fusion.10
  339.4 3.4 dynamic-slice_select_fusion.10
  342.8 2.0 dynamic-update-slice.34
  345.6 2.7 and_reduce_fusion.10
  348.3 3.4 dynamic-slice_select_fusion.10
  351.6 2.1 dynamic-update-slice.34
  355.3 17.7 %while.15 = (s32[]{:T(128)}, f32[2,264,1024]{2,1,0:T(8,128)S(1)}, s32[2,3]{1,0:T(2,128)S(1)}, f32[2,256,1024]{2,1,0:T(8,128)}, s32[]{:T(128)}, /*index=5*/s32[3]{0:T(128)S(1)}, s32[]{:T(128)}) while((s32[]{:T(128)}, f32[2,264,1024]{2,1,0:T(8,128)S(1)}, s32[2,3]{1,0:T(2,128)S(1)}, f32[2,256,1024]{2,1,0:T(8,128)}, s32[]{:T(128)}, ...), condition=%wide.while_cond.7, body=%wide.while_body.7.sunk | while | flops 262163 | bytes 5243051 | solution.py:71
  356.0 2.6 and_reduce_fusion.11
  358.7 3.4 dynamic-slice_select_fusion.11
  362.0 2.1 dynamic-update-slice.35
  364.9 2.6 and_reduce_fusion.11
  367.5 3.4 dynamic-slice_select_fusion.11
  370.9 2.1 dynamic-update-slice.35
  374.7 1.5 copy.75
  376.3 20.1 %reduce-scatter.9.cloned.1.call-done = f32[16,2,8,1024]{3,2,1,0:T(8,128)} async-done(((f32[32,2,8,1024]{3,2,1,0:T(8,128)}), f32[16,2,8,1024]{3,2,1,0:T(8,128)}) %reduce-scatter.9.cloned.1.call-update) | async-done | bytes 1048592 | tf_op jit(solution)/shard_map/reduce_scatter | solution.py:24
  396.6 73.2 %reduce-scatter.11.cloned.1.call-done = f32[1,2,8,1024]{3,2,1,0:T(8,128)} async-done(((f32[16,2,8,1024]{3,2,1,0:T(8,128)}), f32[1,2,8,1024]{3,2,1,0:T(8,128)}) %reduce-scatter.11.cloned.1.call-update) | async-done | bytes 65552 | tf_op jit(solution)/shard_map/reduce_scatter | solution.py:24
  470.7 32.6 %all_gather.23 = bf16[16,2,8,1024]{3,2,1,0:T(8,128)(2,1)} all-gather(bf16[1,2,8,1024]{3,2,1,0:T(8,128)(2,1)S(1)} %fusion.70), channel_id=1, replica_groups=mesh['grp'=2,'slab_0'=16,'slab_1'=2,'ang'=4] {'slab_0'}, dimensions={0}, use_global_device_ids=true | all-gather | bytes 557056 | tf_op jit(solution)/shard_map/all_gather | solution.py:48
  503.4 16.8 %all-gather.7.cloned.1.call-done = bf16[32,2,8,1024]{3,2,1,0:T(8,128)(2,1)} async-done(((bf16[16,2,8,1024]{3,2,1,0:T(8,128)(2,1)}), bf16[32,2,8,1024]{3,2,1,0:T(8,128)(2,1)}) %all-gather.7.cloned.1.call-update) | async-done | bytes 1048592 | tf_op jit(solution)/shard_map/all_gather | solution.py:48
  520.2 1.3 copy.76
  522.5 4.2 fusion.12
  527.3 3.5 add_convert_fusion
  531.0 1.4 collective-permute-start.2
  532.4 46.6 %collective-permute-done.2 = f32[2,256,1024]{2,1,0:T(8,128)S(1)} collective-permute-done((f32[2,256,1024]{2,1,0:T(8,128)S(1)}, f32[2,256,1024]{2,1,0:T(8,128)S(1)}, u32[]{:S(2)}, u32[]{:S(2)}) %collective-permute-start.2) | collective-permute-done | bytes 2097184 | tf_op jit(solution)/shard_map/ppermute | solution.py:98
  579.3 2.2 collective-permute-start.3
  582.2 24.7 %all_to_all.6 = f32[32,1,2]{2,1,0:T(1,128)S(1)} all-to-all(f32[32,1,2]{2,1,0:T(1,128)S(1)} %broadcast_in_dim.7), channel_id=1, replica_groups=mesh['grp'=2,'slab_0'=16,'slab_1'=2,'ang'=4] {'slab_0','slab_1'}, dimensions={0} | all-to-all | bytes 512 | tf_op jit(solution)/shard_map/all_to_all | solution.py:61
  607.5 20.5 %collective-permute-done.3 = f32[2,256,1024]{2,1,0:T(8,128)} collective-permute-done((f32[2,256,1024]{2,1,0:T(8,128)S(1)}, f32[2,256,1024]{2,1,0:T(8,128)}, u32[]{:S(2)}, u32[]{:S(2)}) %collective-permute-start.3) | collective-permute-done | bytes 2097184 | tf_op jit(solution)/shard_map/ppermute | solution.py:98
  628.0 3.2 subtract_convert_fusion
  (119 shorter events, 20.7 us)
Async XLA Ops:
  7.2 89.1 %copy-start = (f32[2,8,1024]{2,1,0:T(8,128)S(1)}, f32[2,8,1024]{2,1,0:T(8,128)}, u32[]{:S(2)}) copy-start(f32[2,8,1024]{2,1,0:T(8,128)} %param.8) | copy-start | bytes 196612
  7.2 88.4 %reduce-scatter.5.cloned.1.call-start = ((), (), s32[]{:S(2)}) async-start(), calls=%async_computation.5 | async-start | bytes 3145728 | tf_op jit(solution)/shard_map/reduce_scatter | solution.py:24
  7.3 4.7 copy-start.5
  7.3 4.7 copy-start.12
  11.9 2.6 copy-start.9
  11.9 2.7 copy-start.10
  14.5 0.7 copy-start.8
  63.0 33.1 %copy-start.11 = (f32[2]{0:T(128)S(1)}, f32[2]{0:T(128)}, u32[]{:S(2)}) copy-start(f32[2]{0:T(128)} %param.9) | copy-start | bytes 28
  63.1 106.0 %reduce-scatter.7.cloned.1.call-start = ((), (), s32[]{:S(2)}) async-start(), calls=%async_computation.6 | async-start | bytes 1114112 | tf_op jit(solution)/shard_map/reduce_scatter | solution.py:24
  95.7 124.9 %all-gather.5.cloned.1.call-start = ((), (), s32[]{:S(2)}) async-start(), calls=%async_computation.9 | async-start | bytes 1572864 | tf_op jit(solution)/shard_map/all_gather | solution.py:48
  204.8 191.6 %reduce-scatter.9.cloned.1.call-start = ((), (), s32[]{:S(2)}) async-start(), calls=%async_computation.7 | async-start | bytes 3145728 | tf_op jit(solution)/shard_map/reduce_scatter | solution.py:24
  231.4 97.0 %copy-start.6 = (bf16[2,256,1024]{2,1,0:T(8,128)(2,1)S(1)}, bf16[2,256,1024]{2,1,0:T(8,128)(2,1)}, u32[]{:S(2)}) copy-start(bf16[2,256,1024]{2,1,0:T(8,128)(2,1)} %param.5) | copy-start | bytes 3145732
  231.4 47.9 %collective-permute-start = (f32[2,256,1024]{2,1,0:T(8,128)S(1)}, f32[2,256,1024]{2,1,0:T(8,128)S(1)}, u32[]{:S(2)}, u32[]{:S(2)}) collective-permute-start(f32[2,256,1024]{2,1,0:T(8,128)S(1)} %convert_element_type.67), channel_id=1, source_target_pairs={{0,1},{1,0},{2,3},{3,2},{4,5},{5,4},{6,7},{7,6},{8,9},{9,8},{10,11... | collective-permute-start | bytes 6291464 | tf_op jit(solution)/shard_map/ppermute | solution.py:98
  279.7 48.7 %collective-permute-start.1 = (f32[2,256,1024]{2,1,0:T(8,128)S(1)}, f32[2,256,1024]{2,1,0:T(8,128)}, u32[]{:S(2)}, u32[]{:S(2)}) collective-permute-start(f32[2,256,1024]{2,1,0:T(8,128)S(1)} %convert_add_fusion.1), channel_id=1, source_target_pairs={{0,2},{1,3},{2,0},{3,1},{4,6},{5,7},{6,4},{7,5},{8,10},{9,11},{10,... | collective-permute-start | bytes 6291464 | tf_op jit(solution)/shard_map/ppermute | solution.py:98
  281.9 48.7 %copy-start.13 = (bf16[2,1024,1024]{2,1,0:T(8,128)(2,1)S(1)}, bf16[2,1024,1024]{2,1,0:T(8,128)(2,1)}, u32[]{:S(2)}) copy-start(bf16[2,1024,1024]{2,1,0:T(8,128)(2,1)} %param.6) | copy-start | bytes 12582916
  330.6 2.6 copy-start.3
  373.3 1.2 copy-start.2
  376.3 93.6 %reduce-scatter.11.cloned.1.call-start = ((), (), s32[]{:S(2)}) async-start(), calls=%async_computation.8 | async-start | bytes 1114112 | tf_op jit(solution)/shard_map/reduce_scatter | solution.py:24
  396.5 123.7 %all-gather.7.cloned.1.call-start = ((), (), s32[]{:S(2)}) async-start(), calls=%async_computation.10 | async-start | bytes 1572864 | tf_op jit(solution)/shard_map/all_gather | solution.py:48
  531.0 50.5 %copy-start.7 = (f32[1,2,8,1024]{3,2,1,0:T(8,128)S(1)}, f32[1,2,8,1024]{3,2,1,0:T(8,128)}, u32[]{:S(2)}) copy-start(f32[1,2,8,1024]{3,2,1,0:T(8,128)} %reduce-scatter.11.cloned.1.call-done) | copy-start | bytes 196612
  531.0 97.0 %copy-start.4 = (bf16[2,256,1024]{2,1,0:T(8,128)(2,1)S(1)}, bf16[2,256,1024]{2,1,0:T(8,128)(2,1)}, u32[]{:S(2)}) copy-start(bf16[2,256,1024]{2,1,0:T(8,128)(2,1)} %copy-done.3) | copy-start | bytes 3145732
  531.0 48.0 %collective-permute-start.2 = (f32[2,256,1024]{2,1,0:T(8,128)S(1)}, f32[2,256,1024]{2,1,0:T(8,128)S(1)}, u32[]{:S(2)}, u32[]{:S(2)}) collective-permute-start(f32[2,256,1024]{2,1,0:T(8,128)S(1)} %convert_element_type.73), channel_id=1, source_target_pairs={{0,1},{1,0},{2,3},{3,2},{4,5},{5,4},{6,7},{7,6},{8,9},{9,8},{10,11... | collective-permute-start | bytes 6291464 | tf_op jit(solution)/shard_map/ppermute | solution.py:98
  579.3 48.7 %collective-permute-start.3 = (f32[2,256,1024]{2,1,0:T(8,128)S(1)}, f32[2,256,1024]{2,1,0:T(8,128)}, u32[]{:S(2)}, u32[]{:S(2)}) collective-permute-start(f32[2,256,1024]{2,1,0:T(8,128)S(1)} %convert_add_fusion), channel_id=1, source_target_pairs={{0,2},{1,3},{2,0},{3,1},{4,6},{5,7},{6,4},{7,5},{8,10},{9,11},{10,... | collective-permute-start | bytes 6291464 | tf_op jit(solution)/shard_map/ppermute | solution.py:98
  607.0 24.2 %copy-start.1 = (f32[2,8,1024]{2,1,0:T(8,128)S(1)}, f32[2,8,1024]{2,1,0:T(8,128)}, u32[]{:S(2)}) copy-start(f32[2,8,1024]{2,1,0:T(8,128)} %param.8) | copy-start | bytes 196612
Sparse Core Ops, SparseCore 0:
  63.2 32.4 reduce-scatter.4
  98.2 70.8 reduce-scatter.6
  205.0 15.6 all-gather.4
  376.4 20.0 reduce-scatter.8
  398.9 70.9 reduce-scatter.10
  503.5 16.6 all-gather.6
